TPU v7x, 512 devices: a whole 4x4x16 slice. The times are simulated.
512 devices in a mesh: sector: 32 (over y, x, core), term: 16 (over z).
Axes of the slice: x: 4, y: 4, z: 16, core: 2. Of those that a mesh axis runs over, the one named last changes fastest.
Arguments:
- blocks: bfloat16 [20480, 640], P('sector'), may hold values from -6 to 6
- left_env: bfloat16 [32, 16, 640, 1920], P('sector', 'term'), may hold values from -0.125 to 0.125
- right_env: bfloat16 [32, 16, 640, 640], P('sector', 'term'), may hold values from -0.0625 to 0.0625
- coupling: int32 [32, 3], P('sector'), may hold values 0 or 1
- widths: int32 [32], P('sector'), may hold values from 320 to 640
Outputs:
- filtered: bfloat16 [20480, 640], P('sector')
All inputs are finite; a program needn't handle non-finite values. No bound on the sum of `coupling` on one device may be relied on, other than what follows from the above.
Results may differ from a plain program's by a relative error of at most 0.005.
Values may be sent and summed in bfloat16 or wider, within the bound.
No kernel may reach another device: no remote copies, remote signals or barrier semaphores. Data moves between devices by JAX's collectives and lax.ppermute only.
A program may use at most 64 MiB of HBM per device.

v0:
```python
import jax
import jax.numpy as jnp
from jax import lax
from jax.sharding import PartitionSpec as P


def with_halo(x, axis):
    count = lax.axis_size(axis)
    up = [(i, (i + 1) % count) for i in range(count - 1)]
    down = [(j, i) for i, j in up]
    before = lax.ppermute(x, axis, up)
    after = lax.ppermute(x, axis, down)
    return jnp.concatenate([before, x, after], axis=0)


def keep_live(values, live_width, row_offset):
    row_index = row_offset + lax.broadcasted_iota(jnp.int32, values.shape, 0)
    col_index = lax.broadcasted_iota(jnp.int32, values.shape, 1)
    return jnp.where(
        (row_index < live_width) & (col_index < live_width), values, jnp.zeros_like(values)
    )


def contract(stacked, left_part, right_part):
    partial_value = jnp.einsum(
        "ik,kj->ij", left_part, stacked, preferred_element_type=jnp.float32
    ).astype(jnp.bfloat16)
    return jnp.einsum("ij,jl->il", partial_value, right_part, preferred_element_type=jnp.float32)


def shards(blocks, left_env, right_env, coupling, widths):
    side = blocks.shape[1]
    left_part = left_env[0, 0]
    right_part = right_env[0, 0]
    live_width = widths[0]
    row_scale = jnp.repeat(coupling[0].astype(jnp.bfloat16), side)
    terms = lax.axis_size("term")
    rows = side // terms
    row_offset = lax.axis_index("term") * rows

    def apply_rows(source):
        nearby = with_halo(source, "sector")
        part = contract(nearby * row_scale[:, None], left_part, right_part)
        part = part.astype(jnp.bfloat16).reshape(terms, rows, side)
        pieces = lax.all_to_all(part, "term", 0, 0, tiled=True)
        total = jnp.sum(pieces.astype(jnp.float32), axis=0)
        return keep_live(total, live_width, row_offset)

    def gather(piece):
        return lax.all_gather(piece, "term", axis=0, tiled=True)

    first_pass = gather(apply_rows(blocks).astype(jnp.bfloat16))
    own = lax.dynamic_slice_in_dim(blocks, row_offset, rows, axis=0).astype(jnp.float32)
    return gather((2.0 * apply_rows(first_pass) - own).astype(jnp.bfloat16))


def solution(mesh):
    placed = (
        P("sector", None),
        P("sector", "term", None, None),
        P("sector", "term", None, None),
        P("sector", None),
        P("sector"),
    )
    return jax.shard_map(
        shards, mesh=mesh, in_specs=placed, out_specs=P("sector", None), check_vma=False
    )
```

profile of v0, /device:TPU:22, one launch (start us, length us, event | category | flops | bytes accessed | tf_op | source)
XLA Modules:
  0.0 220.3 jit_solution(6024967086172461485)
XLA Ops:
  0.0 2.3 %collective-permute-start.1 = (bf16[640,640]{1,0:T(8,128)(2,1)}, bf16[640,640]{1,0:T(8,128)(2,1)S(1)}, u32[]{:S(2)}, u32[]{:S(2)}) collective-permute-start(bf16[640,640]{1,0:T(8,128)(2,1)} %param.5), channel_id=1, source_target_pairs={{16,0},{32,16},{48,32},{64,48},{80,64},{96,80},{112,96},{128,112},... | collective-permute-start | bytes 2457608 | tf_op jit(solution)/shard_map/ppermute | solution.py:12
  2.3 2.2 collective-permute-start
  4.5 0.7 convert_bitcast_fusion
  5.1 0.1 broadcast_in_dim.3
  5.2 7.2 %collective-permute-done.1 = bf16[640,640]{1,0:T(8,128)(2,1)S(1)} collective-permute-done((bf16[640,640]{1,0:T(8,128)(2,1)}, bf16[640,640]{1,0:T(8,128)(2,1)S(1)}, u32[]{:S(2)}, u32[]{:S(2)}) %collective-permute-start.1) | collective-permute-done | bytes 819232 | tf_op jit(solution)/shard_map/ppermute | solution.py:12
  12.5 3.8 %collective-permute-done = bf16[640,640]{1,0:T(8,128)(2,1)} collective-permute-done((bf16[640,640]{1,0:T(8,128)(2,1)}, bf16[640,640]{1,0:T(8,128)(2,1)}, u32[]{:S(2)}, u32[]{:S(2)}) %collective-permute-start) | collective-permute-done | bytes 819232 | tf_op jit(solution)/shard_map/ppermute | solution.py:11
  16.3 6.7 %convolution_convert_fusion.1 = bf16[640,640]{1,0:T(8,128)(2,1)} fusion(bf16[1,1,640,1920]{3,2,1,0:T(8,128)(2,1)S(1)} %copy-done, bf16[640,640]{1,0:T(8,128)(2,1)S(1)} %collective-permute-done.1, bf16[640,640]{1,0:T(8,128)(2,1)} %param.5, bf16[640,640]{1,0:T(8,128)(2,1)} %collective-permute-done, bf16[1920]{0:T(1024)(128)(2,1)S(1)} %mul.26, ...), kind=kOutput, calls=%fused_computation.19 | convolution fusion | flops 2107801600 | bytes 6557440 | tf_op jit(solution)/shard_map/ij,jl->il/dot_general | solution.py:28
  23.0 15.2 %all-to-all-start = ((bf16[16,40,640]{2,1,0:T(8,128)(2,1)}), bf16[16,40,640]{2,1,0:T(8,128)(2,1)S(1)}, u32[]{:S(2)}, u32[]{:S(2)}) async-start(bf16[16,40,640]{2,1,0:T(8,128)(2,1)} %bitcast.25), calls=%async_computation | async-start | bytes 1638400 | tf_op jit(solution)/shard_map/all_to_all | solution.py:45
  38.9 40.2 %all-to-all-done = bf16[16,40,640]{2,1,0:T(8,128)(2,1)S(1)} async-done(((bf16[16,40,640]{2,1,0:T(8,128)(2,1)}), bf16[16,40,640]{2,1,0:T(8,128)(2,1)S(1)}, u32[]{:S(2)}, u32[]{:S(2)}) %all-to-all-start) | async-done | bytes 819232 | tf_op jit(solution)/shard_map/all_to_all | solution.py:45
  79.1 0.1 convert_reduce_fusion.1
  79.2 0.1 fusion.26
  79.3 36.7 %all_gather.6 = bf16[640,640]{1,0:T(8,128)(2,1)S(1)} all-gather(bf16[40,640]{1,0:T(8,128)(2,1)S(1)} %fusion.26), channel_id=1, replica_groups=mesh['sector'=32,'term'=16] {'term'}, dimensions={0}, use_global_device_ids=true | all-gather | bytes 870400 | tf_op jit(solution)/shard_map/all_gather | solution.py:50
  116.0 1.9 collective-permute-start.3
  117.9 2.4 %collective-permute-start.2 = (bf16[640,640]{1,0:T(8,128)(2,1)S(1)}, bf16[640,640]{1,0:T(8,128)(2,1)}, u32[]{:S(2)}, u32[]{:S(2)}) collective-permute-start(bf16[640,640]{1,0:T(8,128)(2,1)S(1)} %all_gather.6), channel_id=1, source_target_pairs={{0,16},{16,32},{32,48},{48,64},{64,80},{80,96},{96,112},{112,128},... | collective-permute-start | bytes 2457608 | tf_op jit(solution)/shard_map/ppermute | solution.py:11
  120.3 7.4 %collective-permute-done.3 = bf16[640,640]{1,0:T(8,128)(2,1)S(1)} collective-permute-done((bf16[640,640]{1,0:T(8,128)(2,1)S(1)}, bf16[640,640]{1,0:T(8,128)(2,1)S(1)}, u32[]{:S(2)}, u32[]{:S(2)}) %collective-permute-start.3) | collective-permute-done | bytes 819232 | tf_op jit(solution)/shard_map/ppermute | solution.py:12
  127.7 0.9 copy-done.1
  128.6 3.0 %collective-permute-done.2 = bf16[640,640]{1,0:T(8,128)(2,1)} collective-permute-done((bf16[640,640]{1,0:T(8,128)(2,1)S(1)}, bf16[640,640]{1,0:T(8,128)(2,1)}, u32[]{:S(2)}, u32[]{:S(2)}) %collective-permute-start.2) | collective-permute-done | bytes 819232 | tf_op jit(solution)/shard_map/ppermute | solution.py:11
  131.7 6.7 %convolution_convert_fusion = bf16[640,640]{1,0:T(8,128)(2,1)} fusion(bf16[1,1,640,1920]{3,2,1,0:T(8,128)(2,1)S(1)} %copy-done, bf16[640,640]{1,0:T(8,128)(2,1)} %copy-done.1, bf16[640,640]{1,0:T(8,128)(2,1)S(1)} %all_gather.6, bf16[640,640]{1,0:T(8,128)(2,1)} %collective-permute-done.2, bf16[1920]{0:T(1024)(128)(2,1)S(1)} %mul.26, ...), kind=kOutput, calls=%fused_computation.18 | convolution fusion | flops 2107801600 | bytes 6557440 | tf_op jit(solution)/shard_map/ij,jl->il/dot_general | solution.py:28
  138.4 5.2 %all-to-all-start.1 = ((bf16[16,40,640]{2,1,0:T(8,128)(2,1)}), bf16[16,40,640]{2,1,0:T(8,128)(2,1)S(1)}, u32[]{:S(2)}, u32[]{:S(2)}) async-start(bf16[16,40,640]{2,1,0:T(8,128)(2,1)} %bitcast.26), calls=%async_computation.1 | async-start | bytes 1638400 | tf_op jit(solution)/shard_map/all_to_all | solution.py:45
  143.6 37.5 %all-to-all-done.1 = bf16[16,40,640]{2,1,0:T(8,128)(2,1)S(1)} async-done(((bf16[16,40,640]{2,1,0:T(8,128)(2,1)}), bf16[16,40,640]{2,1,0:T(8,128)(2,1)S(1)}, u32[]{:S(2)}, u32[]{:S(2)}) %all-to-all-start.1) | async-done | bytes 819232 | tf_op jit(solution)/shard_map/all_to_all | solution.py:45
  181.1 0.1 convert_reduce_fusion
  181.2 0.9 fusion.29
  182.2 37.2 %all_gather.7 = bf16[640,640]{1,0:T(8,128)(2,1)S(1)} all-gather(bf16[40,640]{1,0:T(8,128)(2,1)S(1)} %fusion.29), channel_id=1, replica_groups=mesh['sector'=32,'term'=16] {'term'}, dimensions={0}, use_global_device_ids=true | all-gather | bytes 870400 | tf_op jit(solution)/shard_map/all_gather | solution.py:50
  219.4 0.9 copy.8
  (6 shorter events, 0.0 us)
Async XLA Ops:
  0.0 16.3 %copy-start = (bf16[1,1,640,1920]{3,2,1,0:T(8,128)(2,1)S(1)}, bf16[1,1,640,1920]{3,2,1,0:T(8,128)(2,1)}, u32[]{:S(2)}) copy-start(bf16[1,1,640,1920]{3,2,1,0:T(8,128)(2,1)} %param.6) | copy-start | bytes 7372804
  0.0 12.5 %collective-permute-start.1 = (bf16[640,640]{1,0:T(8,128)(2,1)}, bf16[640,640]{1,0:T(8,128)(2,1)S(1)}, u32[]{:S(2)}, u32[]{:S(2)}) collective-permute-start(bf16[640,640]{1,0:T(8,128)(2,1)} %param.5), channel_id=1, source_target_pairs={{16,0},{32,16},{48,32},{64,48},{80,64},{96,80},{112,96},{128,112},... | collective-permute-start | bytes 2457608 | tf_op jit(solution)/shard_map/ppermute | solution.py:12
  2.3 14.0 %collective-permute-start = (bf16[640,640]{1,0:T(8,128)(2,1)}, bf16[640,640]{1,0:T(8,128)(2,1)}, u32[]{:S(2)}, u32[]{:S(2)}) collective-permute-start(bf16[640,640]{1,0:T(8,128)(2,1)} %param.5), channel_id=1, source_target_pairs={{0,16},{16,32},{32,48},{48,64},{64,80},{80,96},{96,112},{112,128},... | collective-permute-start | bytes 2457608 | tf_op jit(solution)/shard_map/ppermute | solution.py:11
  23.0 56.0 %all-to-all-start = ((bf16[16,40,640]{2,1,0:T(8,128)(2,1)}), bf16[16,40,640]{2,1,0:T(8,128)(2,1)S(1)}, u32[]{:S(2)}, u32[]{:S(2)}) async-start(bf16[16,40,640]{2,1,0:T(8,128)(2,1)} %bitcast.25), calls=%async_computation | async-start | bytes 1638400 | tf_op jit(solution)/shard_map/all_to_all | solution.py:45
  116.0 11.8 %collective-permute-start.3 = (bf16[640,640]{1,0:T(8,128)(2,1)S(1)}, bf16[640,640]{1,0:T(8,128)(2,1)S(1)}, u32[]{:S(2)}, u32[]{:S(2)}) collective-permute-start(bf16[640,640]{1,0:T(8,128)(2,1)S(1)} %all_gather.6), channel_id=1, source_target_pairs={{16,0},{32,16},{48,32},{64,48},{80,64},{96,80},{112,96},{128,112},... | collective-permute-start | bytes 2457608 | tf_op jit(solution)/shard_map/ppermute | solution.py:12
  117.9 13.8 %collective-permute-start.2 = (bf16[640,640]{1,0:T(8,128)(2,1)S(1)}, bf16[640,640]{1,0:T(8,128)(2,1)}, u32[]{:S(2)}, u32[]{:S(2)}) collective-permute-start(bf16[640,640]{1,0:T(8,128)(2,1)S(1)} %all_gather.6), channel_id=1, source_target_pairs={{0,16},{16,32},{32,48},{48,64},{64,80},{80,96},{96,112},{112,128},... | collective-permute-start | bytes 2457608 | tf_op jit(solution)/shard_map/ppermute | solution.py:11
  127.7 0.9 copy-start.1
  138.4 42.7 %all-to-all-start.1 = ((bf16[16,40,640]{2,1,0:T(8,128)(2,1)}), bf16[16,40,640]{2,1,0:T(8,128)(2,1)S(1)}, u32[]{:S(2)}, u32[]{:S(2)}) async-start(bf16[16,40,640]{2,1,0:T(8,128)(2,1)} %bitcast.26), calls=%async_computation.1 | async-start | bytes 1638400 | tf_op jit(solution)/shard_map/all_to_all | solution.py:45
where the time goes:
time: 221 us; the launch traced here: 220 us
  waiting for transfers between devices  99.2 us (45%)
  blocking collectives  74 us (33%)
  starting transfers between devices  29.1 us (13%)
  matrix products  13.5 us (6%)
    all_to_all x2, waiting for transfers between devices, apply_rows(): pieces = lax.all_to_all(part, 'term', 0, 0, tiled=True)  77.7 us
    all_gather x2, blocking collectives, gather(): return lax.all_gather(piece, 'term', axis=0, tiled=True)  74 us
    all_to_all x2, starting transfers between devices, apply_rows(): pieces = lax.all_to_all(part, 'term', 0, 0, tiled=True)  20.4 us
    ppermute x2, waiting for transfers between devices, with_halo(): after = lax.ppermute(x, axis, down)  14.7 us
    dot_general x2, matrix products, contract(): jnp.einsum('ij,jl->il', partial_value, right_part, preferred_element_type...  13.5 us
    ppermute x2, waiting for transfers between devices, with_halo(): before = lax.ppermute(x, axis, up)  6.86 us
    ppermute x2, starting transfers between devices, with_halo(): before = lax.ppermute(x, axis, up)  4.56 us
  transfers between devices with their start and end apart: 6, of which 6 were waited for; matrix products, arithmetic and copies ran while one was open for 0% of the time, Pallas kernels for 0%

commit v1 on v0

--- a/solution.py
+++ b/solution.py
@@ -2,6 +2,13 @@
 import jax.numpy as jnp
 from jax import lax
 from jax.sharding import PartitionSpec as P
+from jax.lax import all_to_all, axis_size
+
+
+def track_turns_now(block_here):
+    axis_tag = "term"
+    big = jnp.concatenate([block_here for _ in range(axis_size(axis_tag))], 0)
+    return all_to_all(big, axis_tag, 0, 0, tiled=True)
 
 
 def with_halo(x, axis):
@@ -47,7 +54,7 @@
         return keep_live(total, live_width, row_offset)
 
     def gather(piece):
-        return lax.all_gather(piece, "term", axis=0, tiled=True)
+        return track_turns_now(piece)
 
     first_pass = gather(apply_rows(blocks).astype(jnp.bfloat16))
     own = lax.dynamic_slice_in_dim(blocks, row_offset, rows, axis=0).astype(jnp.float32)

time: 221 us -> 253 us (1.14)
  blocking collectives: 74 us -> 102 us
  waiting for transfers between devices: 99.2 us -> 103 us
    all_to_all x0 -> x2, blocking collectives: none -> 102 us  [track_turns_now(): return all_to_all(big, axis_tag, 0, 0, tiled=True)]
    all_gather x2 -> x0, blocking collectives: 74 us -> none  [gather(): return lax.all_gather(piece, 'term', axis=0, tiled=True)]
    all_to_all x2, waiting for transfers between devices: 77.7 us -> 81.4 us  [apply_rows(): pieces = lax.all_to_all(part, 'term', 0, 0, tiled=True)]
where the time goes in v1:
time: 253 us
  waiting for transfers between devices  103 us (41%)
  blocking collectives  102 us (40%)
  starting transfers between devices  29.5 us (12%)
  matrix products  13.5 us (5%)
    all_to_all x2, blocking collectives, track_turns_now(): return all_to_all(big, axis_tag, 0, 0, tiled=True)  102 us
    all_to_all x2, waiting for transfers between devices, apply_rows(): pieces = lax.all_to_all(part, 'term', 0, 0, tiled=True)  81.4 us
    all_to_all x2, starting transfers between devices, apply_rows(): pieces = lax.all_to_all(part, 'term', 0, 0, tiled=True)  20.7 us
    ppermute x2, waiting for transfers between devices, with_halo(): after = lax.ppermute(x, axis, down)  14.7 us
    dot_general x2, matrix products, contract(): jnp.einsum('ij,jl->il', partial_value, right_part, preferred_element_type...  13.5 us
    ppermute x2, waiting for transfers between devices, with_halo(): before = lax.ppermute(x, axis, up)  6.86 us
  transfers between devices with their start and end apart: 6, of which 6 were waited for; matrix products, arithmetic and copies ran while one was open for 0% of the time, Pallas kernels for 0%

profile of v1, /device:TPU:22, one launch (start us, length us, event | category | flops | bytes accessed | tf_op | source)
XLA Modules:
  0.0 252.6 jit_solution(10730216365307867829)
XLA Ops:
  0.0 2.3 collective-permute-start.1
  2.3 2.2 collective-permute-start
  4.5 0.7 convert_bitcast_fusion
  5.1 0.1 broadcast_in_dim.3
  5.2 7.2 %collective-permute-done.1 = bf16[640,640]{1,0:T(8,128)(2,1)S(1)} collective-permute-done((bf16[640,640]{1,0:T(8,128)(2,1)}, bf16[640,640]{1,0:T(8,128)(2,1)S(1)}, u32[]{:S(2)}, u32[]{:S(2)}) %collective-permute-start.1) | collective-permute-done | bytes 819232 | tf_op jit(solution)/shard_map/ppermute | solution.py:19
  12.5 3.8 %collective-permute-done = bf16[640,640]{1,0:T(8,128)(2,1)} collective-permute-done((bf16[640,640]{1,0:T(8,128)(2,1)}, bf16[640,640]{1,0:T(8,128)(2,1)}, u32[]{:S(2)}, u32[]{:S(2)}) %collective-permute-start) | collective-permute-done | bytes 819232 | tf_op jit(solution)/shard_map/ppermute | solution.py:18
  16.3 6.7 %convolution_convert_fusion.1 = bf16[640,640]{1,0:T(8,128)(2,1)} fusion(bf16[1,1,640,1920]{3,2,1,0:T(8,128)(2,1)S(1)} %copy-done, bf16[640,640]{1,0:T(8,128)(2,1)S(1)} %collective-permute-done.1, bf16[640,640]{1,0:T(8,128)(2,1)} %param.5, bf16[640,640]{1,0:T(8,128)(2,1)} %collective-permute-done, bf16[1920]{0:T(1024)(128)(2,1)S(1)} %mul.26, ...), kind=kOutput, calls=%fused_computation.19 | convolution fusion | flops 2107801600 | bytes 6557440 | tf_op jit(solution)/shard_map/ij,jl->il/dot_general | solution.py:35
  23.0 15.2 %all-to-all-start = ((bf16[16,40,640]{2,1,0:T(8,128)(2,1)}), bf16[16,40,640]{2,1,0:T(8,128)(2,1)S(1)}, u32[]{:S(2)}, u32[]{:S(2)}) async-start(bf16[16,40,640]{2,1,0:T(8,128)(2,1)} %bitcast.32), calls=%async_computation | async-start | bytes 1638400 | tf_op jit(solution)/shard_map/all_to_all | solution.py:52
  38.9 40.2 %all-to-all-done = bf16[16,40,640]{2,1,0:T(8,128)(2,1)S(1)} async-done(((bf16[16,40,640]{2,1,0:T(8,128)(2,1)}), bf16[16,40,640]{2,1,0:T(8,128)(2,1)S(1)}, u32[]{:S(2)}, u32[]{:S(2)}) %all-to-all-start) | async-done | bytes 819232 | tf_op jit(solution)/shard_map/all_to_all | solution.py:52
  79.1 0.1 convert_reduce_fusion.1
  79.2 0.1 constant_dynamic-update-slice_fusion.15
  79.5 50.9 %all_to_all.34 = bf16[16,40,640]{2,1,0:T(8,128)(2,1)S(1)} all-to-all(bf16[16,40,640]{2,1,0:T(8,128)(2,1)S(1)} %bitcast.30), channel_id=1, replica_groups=mesh['sector'=32,'term'=16] {'term'}, dimensions={0} | all-to-all | bytes 1638400 | tf_op jit(solution)/shard_map/all_to_all | solution.py:11
  130.4 1.9 collective-permute-start.3
  132.3 2.4 collective-permute-start.2
  134.7 7.4 %collective-permute-done.3 = bf16[640,640]{1,0:T(8,128)(2,1)S(1)} collective-permute-done((bf16[640,640]{1,0:T(8,128)(2,1)S(1)}, bf16[640,640]{1,0:T(8,128)(2,1)S(1)}, u32[]{:S(2)}, u32[]{:S(2)}) %collective-permute-start.3) | collective-permute-done | bytes 819232 | tf_op jit(solution)/shard_map/ppermute | solution.py:19
  142.1 0.9 copy-done.1
  143.0 3.0 %collective-permute-done.2 = bf16[640,640]{1,0:T(8,128)(2,1)} collective-permute-done((bf16[640,640]{1,0:T(8,128)(2,1)S(1)}, bf16[640,640]{1,0:T(8,128)(2,1)}, u32[]{:S(2)}, u32[]{:S(2)}) %collective-permute-start.2) | collective-permute-done | bytes 819232 | tf_op jit(solution)/shard_map/ppermute | solution.py:18
  146.1 6.8 %convolution_convert_fusion = bf16[640,640]{1,0:T(8,128)(2,1)} fusion(bf16[1,1,640,1920]{3,2,1,0:T(8,128)(2,1)S(1)} %copy-done, bf16[640,640]{1,0:T(8,128)(2,1)} %copy-done.1, bf16[640,640]{1,0:T(8,128)(2,1)S(1)} %bitcast.35, bf16[640,640]{1,0:T(8,128)(2,1)} %collective-permute-done.2, bf16[1920]{0:T(1024)(128)(2,1)S(1)} %mul.26, ...), kind=kOutput, calls=%fused_computation.18 | convolution fusion | flops 2107801600 | bytes 6557440 | tf_op jit(solution)/shard_map/ij,jl->il/dot_general | solution.py:35
  152.8 5.5 %all-to-all-start.2 = ((bf16[16,40,640]{2,1,0:T(8,128)(2,1)}), bf16[16,40,640]{2,1,0:T(8,128)(2,1)S(1)}, u32[]{:S(2)}, u32[]{:S(2)}) async-start(bf16[16,40,640]{2,1,0:T(8,128)(2,1)} %bitcast.36), calls=%async_computation.2 | async-start | bytes 1638400 | tf_op jit(solution)/shard_map/all_to_all | solution.py:52
  158.4 41.2 %all-to-all-done.2 = bf16[16,40,640]{2,1,0:T(8,128)(2,1)S(1)} async-done(((bf16[16,40,640]{2,1,0:T(8,128)(2,1)}), bf16[16,40,640]{2,1,0:T(8,128)(2,1)S(1)}, u32[]{:S(2)}, u32[]{:S(2)}) %all-to-all-start.2) | async-done | bytes 819232 | tf_op jit(solution)/shard_map/all_to_all | solution.py:52
  199.6 0.1 convert_reduce_fusion
  199.7 0.9 constant_dynamic-update-slice_fusion.31
  200.9 50.8 %all_to_all.35 = bf16[16,40,640]{2,1,0:T(8,128)(2,1)S(1)} all-to-all(bf16[16,40,640]{2,1,0:T(8,128)(2,1)S(1)} %bitcast.31), channel_id=1, replica_groups=mesh['sector'=32,'term'=16] {'term'}, dimensions={0} | all-to-all | bytes 1638400 | tf_op jit(solution)/shard_map/all_to_all | solution.py:11
  251.7 0.9 copy.38
  (36 shorter events, 0.4 us)
Async XLA Ops:
  0.0 16.3 %copy-start = (bf16[1,1,640,1920]{3,2,1,0:T(8,128)(2,1)S(1)}, bf16[1,1,640,1920]{3,2,1,0:T(8,128)(2,1)}, u32[]{:S(2)}) copy-start(bf16[1,1,640,1920]{3,2,1,0:T(8,128)(2,1)} %param.6) | copy-start | bytes 7372804
  0.0 12.5 %collective-permute-start.1 = (bf16[640,640]{1,0:T(8,128)(2,1)}, bf16[640,640]{1,0:T(8,128)(2,1)S(1)}, u32[]{:S(2)}, u32[]{:S(2)}) collective-permute-start(bf16[640,640]{1,0:T(8,128)(2,1)} %param.5), channel_id=1, source_target_pairs={{16,0},{32,16},{48,32},{64,48},{80,64},{96,80},{112,96},{128,112},... | collective-permute-start | bytes 2457608 | tf_op jit(solution)/shard_map/ppermute | solution.py:19
  2.3 14.0 %collective-permute-start = (bf16[640,640]{1,0:T(8,128)(2,1)}, bf16[640,640]{1,0:T(8,128)(2,1)}, u32[]{:S(2)}, u32[]{:S(2)}) collective-permute-start(bf16[640,640]{1,0:T(8,128)(2,1)} %param.5), channel_id=1, source_target_pairs={{0,16},{16,32},{32,48},{48,64},{64,80},{80,96},{96,112},{112,128},... | collective-permute-start | bytes 2457608 | tf_op jit(solution)/shard_map/ppermute | solution.py:18
  23.0 56.0 %all-to-all-start = ((bf16[16,40,640]{2,1,0:T(8,128)(2,1)}), bf16[16,40,640]{2,1,0:T(8,128)(2,1)S(1)}, u32[]{:S(2)}, u32[]{:S(2)}) async-start(bf16[16,40,640]{2,1,0:T(8,128)(2,1)} %bitcast.32), calls=%async_computation | async-start | bytes 1638400 | tf_op jit(solution)/shard_map/all_to_all | solution.py:52
  130.4 11.8 %collective-permute-start.3 = (bf16[640,640]{1,0:T(8,128)(2,1)S(1)}, bf16[640,640]{1,0:T(8,128)(2,1)S(1)}, u32[]{:S(2)}, u32[]{:S(2)}) collective-permute-start(bf16[640,640]{1,0:T(8,128)(2,1)S(1)} %bitcast.33), channel_id=1, source_target_pairs={{16,0},{32,16},{48,32},{64,48},{80,64},{96,80},{112,96},{128,112},... | collective-permute-start | bytes 2457608 | tf_op jit(solution)/shard_map/ppermute | solution.py:19
  132.3 13.8 %collective-permute-start.2 = (bf16[640,640]{1,0:T(8,128)(2,1)S(1)}, bf16[640,640]{1,0:T(8,128)(2,1)}, u32[]{:S(2)}, u32[]{:S(2)}) collective-permute-start(bf16[640,640]{1,0:T(8,128)(2,1)S(1)} %bitcast.34), channel_id=1, source_target_pairs={{0,16},{16,32},{32,48},{48,64},{64,80},{80,96},{96,112},{112,128},... | collective-permute-start | bytes 2457608 | tf_op jit(solution)/shard_map/ppermute | solution.py:18
  142.1 0.9 copy-start.1
  152.8 46.8 %all-to-all-start.2 = ((bf16[16,40,640]{2,1,0:T(8,128)(2,1)}), bf16[16,40,640]{2,1,0:T(8,128)(2,1)S(1)}, u32[]{:S(2)}, u32[]{:S(2)}) async-start(bf16[16,40,640]{2,1,0:T(8,128)(2,1)} %bitcast.36), calls=%async_computation.2 | async-start | bytes 1638400 | tf_op jit(solution)/shard_map/all_to_all | solution.py:52
